TPU v7x, 16 devices: a 4x2x1 block of a 4x4x8 slice. The times are simulated.
16 devices in a mesh: rep: 4 (over y, z, core), pp: 4 (over x).
Axes of the slice: x: 4, y: 2, z: 1, core: 2. Of those that a mesh axis runs over, the one named last changes fastest.
The devices are a block of a 4x4x8 slice.
Arguments:
- x: bfloat16 [32, 512, 512], P('rep'), parts along dimension 0
- dy: bfloat16 [32, 512, 512], P('rep'), parts along dimension 0
- w_gate: bfloat16 [4, 512, 1792], P('pp')
- w_up: bfloat16 [4, 512, 1792], P('pp')
- w_down: bfloat16 [4, 1792, 512], P('pp')
Outputs:
- output 1: bfloat16 [16, 512, 1792], P(('rep', 'pp')), parts along dimension 0
- output 2: bfloat16 [16, 512, 1792], P(('rep', 'pp')), parts along dimension 0
- output 3: bfloat16 [16, 1792, 512], P(('rep', 'pp')), parts along dimension 0
There are 4 independent parts. A program takes and returns all parts, laid end to end along the dimension named above; an argument that names none is the same for every part.
All inputs are finite; a program needn't handle non-finite values.
Results may differ from a plain program's by a relative error of at most 0.018.
Values are sent between devices in bfloat16 or wider.
A program may use at most 768 MiB of HBM per device.

v0:
```python
import functools

import jax
import jax.numpy as jnp
from jax import lax
from jax.experimental import pallas as pl
from jax.experimental.pallas import tpu as pltpu
from jax.sharding import PartitionSpec as P

ROWS = 128
COLS = 256
LAG = 4
MESH = pl.DeviceIdType.MESH
F32, BF16 = jnp.float32, jnp.bfloat16


def dot(a, b):
    return jnp.dot(a, b, preferred_element_type=F32)


def kernel(
    stages, pieces,
    x, dy, wg_in, wu_in, wd_in,
    og, ou, od,
    wg, wu, wd, wgt, wut, wdt, acc_g, acc_u, acc_d,
    h_in, d_in, h_out, d_out, act, dg, du, at, byt,
    w_sem, o_sem, rf, rb, sf, sb,
):
    me = lax.axis_index("pp")
    n, rows, d = x.shape
    ff = wg_in.shape[1]
    first, last = me == 0, me == stages - 1
    lag = (stages - 1 - me) * LAG

    def load_x(i):
        return pltpu.make_async_copy(x.at[i], h_in.at[i], rf.at[i])

    def load_dy(i):
        return pltpu.make_async_copy(dy.at[i], d_in.at[i], rb.at[i])

    weights = [
        pltpu.make_async_copy(src, dst, w_sem.at[k]) for k, (src, dst) in enumerate(((wg_in, wg), (wu_in, wu), (wd_in, wd)))
    ]

    @pl.when(first)
    def _():
        load_x(0).start()

    for w in weights:
        w.start()

    @pl.when(first)
    def _():
        lax.fori_loop(1, n, lambda i, c: (load_x(i).start(), c)[1], 0)

    @pl.when(last)
    def _():
        lax.fori_loop(0, n, lambda i, c: (load_dy(i).start(), c)[1], 0)

    def onward(i):
        return pltpu.make_async_remote_copy(
            src_ref=h_out.at[i], dst_ref=h_in.at[i], send_sem=sf.at[i], recv_sem=rf.at[i],
            device_id={"pp": jnp.minimum(me + 1, stages - 1)}, device_id_type=MESH,
        )

    def back(i):
        return pltpu.make_async_remote_copy(
            src_ref=d_out.at[i], dst_ref=d_in.at[i], send_sem=sb.at[i], recv_sem=rb.at[i],
            device_id={"pp": jnp.maximum(me - 1, 0)}, device_id_type=MESH,
        )

    barrier = pltpu.get_barrier_semaphore()

    @pl.when(me > 0)
    def _():
        pl.semaphore_signal(barrier, inc=1, device_id={"pp": me - 1}, device_id_type=MESH)

    @pl.when(me < stages - 1)
    def _():
        pl.semaphore_signal(barrier, inc=1, device_id={"pp": me + 1}, device_id_type=MESH)

    pl.semaphore_wait(barrier, (me > 0).astype(jnp.int32) + (me < stages - 1).astype(jnp.int32))

    for w in weights:
        w.wait()

    def wait_h(i):
        @pl.when(first)
        def _():
            load_x(i).wait()

        @pl.when(me > 0)
        def _():
            onward(i).wait_recv()

    def wait_d(i):
        @pl.when(last)
        def _():
            load_dy(i).wait()

        @pl.when(me < stages - 1)
        def _():
            back(i).wait_recv()

    def normed(i):
        wide = h_in[i].astype(F32)
        scale = lax.rsqrt(jnp.mean(wide * wide, -1, keepdims=True) + 1e-6)
        return wide, scale, (wide * scale).astype(BF16)

    def forward(i):
        wait_h(i)
        _, _, a = normed(i)
        for j in range(0, ff, COLS):
            cols = pl.ds(j, COLS)
            gate, up = dot(a, wg[:, cols]), dot(a, wu[:, cols])
            act[2, pl.ds(0, rows), cols] = (gate * jax.nn.sigmoid(gate) * up).astype(BF16)
        y = dot(act[2, pl.ds(0, rows), :], wd[...]).astype(BF16)
        h_out[i] = h_in[i] + y
        onward(i).start()

    def backward(i):
        @pl.when(last)
        def _():
            wait_h(i)

        wait_d(i)
        slot, c = lax.rem(lax.div(i, pieces), 2), lax.rem(i, pieces)
        here = pl.ds(pl.multiple_of(c * rows, rows), rows)
        wide, scale, a = normed(i)
        by = d_in[i]
        at[slot, :, here] = a.T
        byt[slot, :, here] = by.T
        for j in range(0, ff, COLS):
            cols = pl.ds(j, COLS)
            gate, up = dot(a, wg[:, cols]), dot(a, wu[:, cols])
            by_act = dot(by, wdt[:, cols]).astype(BF16).astype(F32)
            sg = jax.nn.sigmoid(gate)
            silu = gate * sg
            act[slot, here, cols] = (silu * up).astype(BF16)
            du[slot, here, cols] = (by_act * silu).astype(BF16)
            dg[slot, here, cols] = (by_act * up * (sg + silu * (1.0 - sg))).astype(BF16)

        @pl.when(me > 0)
        def _():
            by_a = dot(dg[slot, here, :], wgt[...]).astype(BF16) + dot(du[slot, here, :], wut[...]).astype(BF16)
            by_a = by_a.astype(F32)
            inner = jnp.sum(by_a * wide, -1, keepdims=True) * (scale * scale * scale) * (1.0 / d)
            d_out[i] = by + (by_a * scale - wide * inner).astype(BF16)
            back(i).start()

    def out_copies(slot, here, p):
        return [
            pltpu.make_async_copy(buf.at[slot, here, :], out.at[here, :], o_sem.at[k, p])
            for k, (buf, out) in enumerate(((dg, og), (du, ou), (act, od)))
        ]

    def weigh(i):
        m, p = lax.div(i, pieces), lax.rem(i, pieces)
        slot = lax.rem(m, 2)
        here = pl.ds(pl.multiple_of(p * (d // pieces), d // pieces), d // pieces)
        for left, right, acc in ((at, dg, acc_g), (at, du, acc_u), (byt, act, acc_d)):
            lhs = left[slot, here, :]
            for j in range(0, ff, COLS):
                cols = pl.ds(j, COLS)
                acc[here, cols] += dot(lhs, right[slot, :, cols]).astype(BF16).astype(F32)

        @pl.when(i >= n - pieces)
        def _():
            for acc, buf in ((acc_g, dg), (acc_u, du), (acc_d, act)):
                buf[1 - slot, here, :] = acc[here, :].astype(BF16)
            for copy in out_copies(1 - slot, here, p):
                copy.start()

    def step(i, carry):
        @pl.when((me < stages - 1) & (i < n))
        def _():
            forward(i)

        @pl.when(i == jnp.where(first, 1, 0))
        def _():
            for j in range(0, ff, COLS):
                wdt[:, j : j + COLS] = wd[j : j + COLS, :].T
            for acc in (acc_g, acc_u, acc_d):
                acc[...] = jnp.zeros_like(acc)

            @pl.when(me > 0)
            def _():
                for j in range(0, ff, COLS):
                    wgt[j : j + COLS, :] = wg[:, j : j + COLS].T
                    wut[j : j + COLS, :] = wu[:, j : j + COLS].T

        ib = i - lag

        @pl.when((ib >= 0) & (ib < n))
        def _():
            backward(ib)

        @pl.when(ib >= pieces)
        def _():
            weigh(ib - pieces)

        return carry

    lax.fori_loop(0, n + lag + pieces, step, 0)

    @pl.when(me < stages - 1)
    def _():
        lax.fori_loop(0, n, lambda i, c: (onward(i).wait_send(), c)[1], 0)

    @pl.when(me > 0)
    def _():
        lax.fori_loop(0, n, lambda i, c: (back(i).wait_send(), c)[1], 0)

    free = (n // pieces) % 2
    for p in range(pieces):
        for copy in out_copies(free, pl.ds(p * (d // pieces), d // pieces), p):
            copy.wait()


def solution(mesh):
    stages = mesh.shape["pp"]

    def step(x, dy, w_gate, w_up, w_down):
        micro, tokens, d = x.shape
        ff = w_gate.shape[2]
        pieces = tokens // ROWS
        n = micro * pieces
        chunks = lambda v: v.reshape(n, ROWS, d)
        vmem = lambda *shape, dtype=BF16: pltpu.VMEM(shape, dtype)
        sems = lambda *shape: pltpu.SemaphoreType.DMA(shape)
        og, ou, od = pl.pallas_call(
            functools.partial(kernel, stages, pieces),
            name="pipeline",
            out_shape=[jax.ShapeDtypeStruct((d, ff), BF16)] * 3,
            in_specs=[pl.BlockSpec(memory_space=pltpu.HBM)] * 5,
            out_specs=[pl.BlockSpec(memory_space=pltpu.HBM)] * 3,
            scratch_shapes=[
                vmem(d, ff), vmem(d, ff), vmem(ff, d), vmem(ff, d), vmem(ff, d), vmem(d, ff),
                *[vmem(d, ff, dtype=F32)] * 3,
                *[vmem(n, ROWS, d)] * 4,
                vmem(3, tokens, ff), vmem(2, tokens, ff), vmem(2, tokens, ff),
                vmem(2, d, tokens), vmem(2, d, tokens),
                sems(3), sems(3, pieces), sems(n), sems(n), sems(n), sems(n),
            ],
            compiler_params=pltpu.CompilerParams(collective_id=0, has_side_effects=True, vmem_limit_bytes=66_000_000),
        )(chunks(x), chunks(dy), w_gate[0], w_up[0], w_down[0])
        return og[None], ou[None], od.T[None]

    return jax.shard_map(
        step,
        mesh=mesh,
        in_specs=(P("rep", None, None),) * 2 + (P("pp", None, None),) * 3,
        out_specs=(P(("rep", "pp"), None, None),) * 3,
        check_vma=False,
    )
```

profile of v0, /device:TPU:120, one launch (start us, length us, event | category | flops | bytes accessed | tf_op | source)
XLA Modules:
  0.0 163.6 jit_solution(9511759153624403031)
XLA Ops:
  0.6 155.6 %pipeline.1 = (bf16[512,1792]{1,0:T(8,128)(2,1)}, bf16[512,1792]{1,0:T(8,128)(2,1)}, bf16[512,1792]{1,0:T(8,128)(2,1)}) custom-call(bf16[32,128,512]{2,1,0:T(8,128)(2,1)} %bitcast.10, bf16[32,128,512]{2,1,0:T(8,128)(2,1)} %bitcast.11, bf16[512,1792]{1,0:T(8,128)(2,1)} %bitcast.15, bf16[512,1792]{1,0:T(8,128)(2,1)} %bitcast.16, bf16[1792,512]{1,0:T(8,128)(2,1)} %bitcast.17), custom_call_target="tpu_custom_call" | custom-call | tf_op jit(solution)/shard_map/pipeline/pallas_call | solution.py:231
  156.2 0.0 copy-start.1
  156.2 4.0 %copy.8 = bf16[1,1792,512]{2,1,0:T(8,128)(2,1)} copy(bf16[1,1792,512]{1,2,0:T(8,128)(2,1)} %bitcast.14) | data formatting | bytes 3670016
  160.2 0.0 copy-done.1
  160.2 0.0 copy-start
  160.2 1.2 copy.11
  161.4 0.9 copy-done
  162.3 1.2 copy.12
Async XLA Ops:
  156.2 4.0 %copy-start.1 = (bf16[512,1792]{1,0:T(8,128)(2,1)S(1)}, bf16[512,1792]{1,0:T(8,128)(2,1)}, u32[]{:S(2)}) copy-start(bf16[512,1792]{1,0:T(8,128)(2,1)} %get-tuple-element.6) | copy-start | bytes 5505028
  160.2 2.2 %copy-start = (bf16[512,1792]{1,0:T(8,128)(2,1)S(1)}, bf16[512,1792]{1,0:T(8,128)(2,1)}, u32[]{:S(2)}) copy-start(bf16[512,1792]{1,0:T(8,128)(2,1)} %get-tuple-element.7) | copy-start | bytes 5505028
where the time goes:
time: 164 us
  Pallas kernels  156 us (95%)
  local copies, waits for them, and re-layouts  7.36 us (4%)
    pallas_call x1, Pallas kernels, step(): pl.pallas_call(functools.partial(kernel, stages, pieces), name='pipeline'...  156 us
    unnamed x7, local copies, waits for them, and re-layouts  7.36 us

commit v1 on v0

--- a/solution.py
+++ b/solution.py
@@ -8,7 +8,9 @@
 from jax.sharding import PartitionSpec as P
 
 ROWS = 128
+PARTS = 2
 COLS = 256
+RING = 8
 LAG = 4
 MESH = pl.DeviceIdType.MESH
 F32, BF16 = jnp.float32, jnp.bfloat16
@@ -23,13 +25,15 @@
     x, dy, wg_in, wu_in, wd_in,
     og, ou, od,
     wg, wu, wd, wgt, wut, wdt, acc_g, acc_u, acc_d,
-    h_in, d_in, h_out, d_out, act, dg, du, at, byt,
+    h_in, d_in, h_out, d_out, fact, kept_g, kept_u, act, dg, du, at, byt,
     w_sem, o_sem, rf, rb, sf, sb,
 ):
     me = lax.axis_index("pp")
     n, rows, d = x.shape
     ff = wg_in.shape[1]
     first, last = me == 0, me == stages - 1
+    middle = (me > 0) & (me < stages - 1)
+    keeps = kept_g.shape[0]
     lag = (stages - 1 - me) * LAG
 
     def load_x(i):
@@ -59,13 +63,13 @@
 
     def onward(i):
         return pltpu.make_async_remote_copy(
-            src_ref=h_out.at[i], dst_ref=h_in.at[i], send_sem=sf.at[i], recv_sem=rf.at[i],
+            src_ref=h_out.at[lax.rem(i, RING)], dst_ref=h_in.at[i], send_sem=sf.at[i], recv_sem=rf.at[i],
             device_id={"pp": jnp.minimum(me + 1, stages - 1)}, device_id_type=MESH,
         )
 
     def back(i):
         return pltpu.make_async_remote_copy(
-            src_ref=d_out.at[i], dst_ref=d_in.at[i], send_sem=sb.at[i], recv_sem=rb.at[i],
+            src_ref=d_out.at[lax.rem(i, RING)], dst_ref=d_in.at[i], send_sem=sb.at[i], recv_sem=rb.at[i],
             device_id={"pp": jnp.maximum(me - 1, 0)}, device_id_type=MESH,
         )
 
@@ -109,16 +113,24 @@
 
     def forward(i):
         wait_h(i)
+
+        @pl.when(i >= RING)
+        def _():
+            onward(i - RING).wait_send()
+
         _, _, a = normed(i)
+        spot = lax.rem(i, keeps)
         for j in range(0, ff, COLS):
             cols = pl.ds(j, COLS)
             gate, up = dot(a, wg[:, cols]), dot(a, wu[:, cols])
-            act[2, pl.ds(0, rows), cols] = (gate * jax.nn.sigmoid(gate) * up).astype(BF16)
-        y = dot(act[2, pl.ds(0, rows), :], wd[...]).astype(BF16)
-        h_out[i] = h_in[i] + y
+            kept_g[spot, :, cols] = gate
+            kept_u[spot, :, cols] = up
+            fact[:, cols] = (gate * jax.nn.sigmoid(gate) * up).astype(BF16)
+        y = dot(fact[...], wd[...]).astype(BF16)
+        h_out[lax.rem(i, RING)] = h_in[i] + y
         onward(i).start()
 
-    def backward(i):
+    def backward(i, recompute):
         @pl.when(last)
         def _():
             wait_h(i)
@@ -126,13 +138,17 @@
         wait_d(i)
         slot, c = lax.rem(lax.div(i, pieces), 2), lax.rem(i, pieces)
         here = pl.ds(pl.multiple_of(c * rows, rows), rows)
+        spot = lax.rem(i, keeps)
         wide, scale, a = normed(i)
         by = d_in[i]
         at[slot, :, here] = a.T
         byt[slot, :, here] = by.T
         for j in range(0, ff, COLS):
             cols = pl.ds(j, COLS)
-            gate, up = dot(a, wg[:, cols]), dot(a, wu[:, cols])
+            if recompute:
+                gate, up = dot(a, wg[:, cols]), dot(a, wu[:, cols])
+            else:
+                gate, up = kept_g[spot, :, cols], kept_u[spot, :, cols]
             by_act = dot(by, wdt[:, cols]).astype(BF16).astype(F32)
             sg = jax.nn.sigmoid(gate)
             silu = gate * sg
@@ -140,35 +156,40 @@
             du[slot, here, cols] = (by_act * silu).astype(BF16)
             dg[slot, here, cols] = (by_act * up * (sg + silu * (1.0 - sg))).astype(BF16)
 
-        @pl.when(me > 0)
-        def _():
+        def send():
+            @pl.when(i >= RING)
+            def _():
+                back(i - RING).wait_send()
+
             by_a = dot(dg[slot, here, :], wgt[...]).astype(BF16) + dot(du[slot, here, :], wut[...]).astype(BF16)
             by_a = by_a.astype(F32)
             inner = jnp.sum(by_a * wide, -1, keepdims=True) * (scale * scale * scale) * (1.0 / d)
-            d_out[i] = by + (by_a * scale - wide * inner).astype(BF16)
+            d_out[lax.rem(i, RING)] = by + (by_a * scale - wide * inner).astype(BF16)
             back(i).start()
 
-    def out_copies(slot, here, p):
+        pl.when(me > 0)(send) if recompute else send()
+
+    def out_copies(slot, p):
+        here = pl.ds(p * (d // PARTS), d // PARTS)
         return [
             pltpu.make_async_copy(buf.at[slot, here, :], out.at[here, :], o_sem.at[k, p])
             for k, (buf, out) in enumerate(((dg, og), (du, ou), (act, od)))
         ]
 
-    def weigh(i):
-        m, p = lax.div(i, pieces), lax.rem(i, pieces)
+    def weigh(m, p):
         slot = lax.rem(m, 2)
-        here = pl.ds(pl.multiple_of(p * (d // pieces), d // pieces), d // pieces)
+        here = pl.ds(pl.multiple_of(p * (d // PARTS), d // PARTS), d // PARTS)
         for left, right, acc in ((at, dg, acc_g), (at, du, acc_u), (byt, act, acc_d)):
             lhs = left[slot, here, :]
             for j in range(0, ff, COLS):
                 cols = pl.ds(j, COLS)
                 acc[here, cols] += dot(lhs, right[slot, :, cols]).astype(BF16).astype(F32)
 
-        @pl.when(i >= n - pieces)
+        @pl.when(m == n // pieces - 1)
         def _():
             for acc, buf in ((acc_g, dg), (acc_u, du), (acc_d, act)):
                 buf[1 - slot, here, :] = acc[here, :].astype(BF16)
-            for copy in out_copies(1 - slot, here, p):
+            for copy in out_copies(1 - slot, p):
                 copy.start()
 
     def step(i, carry):
@@ -191,13 +212,19 @@
 
         ib = i - lag
 
-        @pl.when((ib >= 0) & (ib < n))
-        def _():
-            backward(ib)
-
-        @pl.when(ib >= pieces)
-        def _():
-            weigh(ib - pieces)
+        @pl.when((ib >= 0) & (ib < n) & middle)
+        def _():
+            backward(ib, False)
+
+        @pl.when((ib >= 0) & (ib < n) & ~middle)
+        def _():
+            backward(ib, True)
+
+        iw, every = ib - pieces, pieces // PARTS
+
+        @pl.when((iw >= 0) & (lax.rem(iw + pieces, every) == every - 1))
+        def _():
+            weigh(lax.div(iw, pieces), lax.div(lax.rem(iw, pieces), every))
 
         return carry
 
@@ -205,15 +232,15 @@
 
     @pl.when(me < stages - 1)
     def _():
-        lax.fori_loop(0, n, lambda i, c: (onward(i).wait_send(), c)[1], 0)
+        lax.fori_loop(n - RING, n, lambda i, c: (onward(i).wait_send(), c)[1], 0)
 
     @pl.when(me > 0)
     def _():
-        lax.fori_loop(0, n, lambda i, c: (back(i).wait_send(), c)[1], 0)
+        lax.fori_loop(n - RING, n, lambda i, c: (back(i).wait_send(), c)[1], 0)
 
     free = (n // pieces) % 2
-    for p in range(pieces):
-        for copy in out_copies(free, pl.ds(p * (d // pieces), d // pieces), p):
+    for p in range(PARTS):
+        for copy in out_copies(free, p):
             copy.wait()
 
 
@@ -237,12 +264,15 @@
             scratch_shapes=[
                 vmem(d, ff), vmem(d, ff), vmem(ff, d), vmem(ff, d), vmem(ff, d), vmem(d, ff),
                 *[vmem(d, ff, dtype=F32)] * 3,
-                *[vmem(n, ROWS, d)] * 4,
-                vmem(3, tokens, ff), vmem(2, tokens, ff), vmem(2, tokens, ff),
+                *[vmem(n, ROWS, d)] * 2,
+                *[vmem(RING, ROWS, d)] * 2,
+                vmem(ROWS, ff),
+                *[vmem(max(stages - 2, 0) * LAG + 1, ROWS, ff, dtype=F32)] * 2,
+                *[vmem(2, tokens, ff)] * 3,
                 vmem(2, d, tokens), vmem(2, d, tokens),
-                sems(3), sems(3, pieces), sems(n), sems(n), sems(n), sems(n),
+                sems(3), sems(3, PARTS), sems(n), sems(n), sems(n), sems(n),
             ],
-            compiler_params=pltpu.CompilerParams(collective_id=0, has_side_effects=True, vmem_limit_bytes=66_000_000),
+            compiler_params=pltpu.CompilerParams(collective_id=0, has_side_effects=True, vmem_limit_bytes=67_000_000),
         )(chunks(x), chunks(dy), w_gate[0], w_up[0], w_down[0])
         return og[None], ou[None], od.T[None]
 

time: 164 us -> 154 us (0.939)
  Pallas kernels: 156 us -> 146 us
    pallas_call x1, Pallas kernels: 156 us -> 146 us  [step(): pl.pallas_call(functools.partial(kernel, stages, pieces), name='pipeline'...]
where the time goes in v1:
time: 154 us
  Pallas kernels  146 us (95%)
  local copies, waits for them, and re-layouts  7.36 us (5%)
    pallas_call x1, Pallas kernels, step(): pl.pallas_call(functools.partial(kernel, stages, pieces), name='pipeline'...  146 us
    unnamed x7, local copies, waits for them, and re-layouts  7.36 us

profile of v1, /device:TPU:120, one launch (start us, length us, event | category | flops | bytes accessed | tf_op | source)
XLA Modules:
  0.0 153.6 jit_solution(12195624398467426250)
XLA Ops:
  0.6 145.6 %pipeline.1 = (bf16[512,1792]{1,0:T(8,128)(2,1)}, bf16[512,1792]{1,0:T(8,128)(2,1)}, bf16[512,1792]{1,0:T(8,128)(2,1)}) custom-call(bf16[32,128,512]{2,1,0:T(8,128)(2,1)} %bitcast.10, bf16[32,128,512]{2,1,0:T(8,128)(2,1)} %bitcast.11, bf16[512,1792]{1,0:T(8,128)(2,1)} %bitcast.15, bf16[512,1792]{1,0:T(8,128)(2,1)} %bitcast.16, bf16[1792,512]{1,0:T(8,128)(2,1)} %bitcast.17), custom_call_target="tpu_custom_call" | custom-call | tf_op jit(solution)/shard_map/pipeline/pallas_call | solution.py:258
  146.2 0.0 copy-start.1
  146.2 4.0 %copy.8 = bf16[1,1792,512]{2,1,0:T(8,128)(2,1)} copy(bf16[1,1792,512]{1,2,0:T(8,128)(2,1)} %bitcast.14) | data formatting | bytes 3670016
  150.2 0.0 copy-done.1
  150.2 0.0 copy-start
  150.2 1.2 copy.11
  151.4 0.9 copy-done
  152.4 1.2 copy.12
Async XLA Ops:
  146.2 4.0 %copy-start.1 = (bf16[512,1792]{1,0:T(8,128)(2,1)S(1)}, bf16[512,1792]{1,0:T(8,128)(2,1)}, u32[]{:S(2)}) copy-start(bf16[512,1792]{1,0:T(8,128)(2,1)} %get-tuple-element.6) | copy-start | bytes 5505028
  150.2 2.2 %copy-start = (bf16[512,1792]{1,0:T(8,128)(2,1)S(1)}, bf16[512,1792]{1,0:T(8,128)(2,1)}, u32[]{:S(2)}) copy-start(bf16[512,1792]{1,0:T(8,128)(2,1)} %get-tuple-element.7) | copy-start | bytes 5505028

commit v2 on v1

--- a/solution.py
+++ b/solution.py
@@ -23,10 +23,10 @@
 def kernel(
     stages, pieces,
     x, dy, wg_in, wu_in, wd_in,
-    og, ou, od,
-    wg, wu, wd, wgt, wut, wdt, acc_g, acc_u, acc_d,
-    h_in, d_in, h_out, d_out, fact, kept_g, kept_u, act, dg, du, at, byt,
-    w_sem, o_sem, rf, rb, sf, sb,
+    wg, wu, wd,
+    wgt, wut, wdt, acc_g, acc_u, acc_d,
+    h_in, d_in, h_out, d_out, kept_g, kept_u, act, dg, du, at, byt,
+    w_sem, rf, rb, sf, sb,
 ):
     me = lax.axis_index("pp")
     n, rows, d = x.shape
@@ -120,17 +120,18 @@
 
         _, _, a = normed(i)
         spot = lax.rem(i, keeps)
+        y = 0.0
         for j in range(0, ff, COLS):
             cols = pl.ds(j, COLS)
             gate, up = dot(a, wg[:, cols]), dot(a, wu[:, cols])
             kept_g[spot, :, cols] = gate
             kept_u[spot, :, cols] = up
-            fact[:, cols] = (gate * jax.nn.sigmoid(gate) * up).astype(BF16)
-        y = dot(fact[...], wd[...]).astype(BF16)
+            y += dot((gate * jax.nn.sigmoid(gate) * up).astype(BF16), wd[cols, :])
+        y = y.astype(BF16)
         h_out[lax.rem(i, RING)] = h_in[i] + y
         onward(i).start()
 
-    def backward(i, recompute):
+    def backward(i, recompute, send):
         @pl.when(last)
         def _():
             wait_h(i)
@@ -139,10 +140,17 @@
         slot, c = lax.rem(lax.div(i, pieces), 2), lax.rem(i, pieces)
         here = pl.ds(pl.multiple_of(c * rows, rows), rows)
         spot = lax.rem(i, keeps)
+        if send:
+
+            @pl.when(i >= RING)
+            def _():
+                back(i - RING).wait_send()
+
         wide, scale, a = normed(i)
         by = d_in[i]
         at[slot, :, here] = a.T
         byt[slot, :, here] = by.T
+        by_a_g, by_a_u = 0.0, 0.0
         for j in range(0, ff, COLS):
             cols = pl.ds(j, COLS)
             if recompute:
@@ -152,52 +160,37 @@
             by_act = dot(by, wdt[:, cols]).astype(BF16).astype(F32)
             sg = jax.nn.sigmoid(gate)
             silu = gate * sg
+            by_up = (by_act * silu).astype(BF16)
+            by_gate = (by_act * up * (sg + silu * (1.0 - sg))).astype(BF16)
             act[slot, here, cols] = (silu * up).astype(BF16)
-            du[slot, here, cols] = (by_act * silu).astype(BF16)
-            dg[slot, here, cols] = (by_act * up * (sg + silu * (1.0 - sg))).astype(BF16)
-
-        def send():
-            @pl.when(i >= RING)
-            def _():
-                back(i - RING).wait_send()
-
-            by_a = dot(dg[slot, here, :], wgt[...]).astype(BF16) + dot(du[slot, here, :], wut[...]).astype(BF16)
-            by_a = by_a.astype(F32)
+            du[slot, here, cols] = by_up
+            dg[slot, here, cols] = by_gate
+            if send:
+                by_a_g += dot(by_gate, wgt[cols, :])
+                by_a_u += dot(by_up, wut[cols, :])
+        if send:
+            by_a = (by_a_g.astype(BF16) + by_a_u.astype(BF16)).astype(F32)
             inner = jnp.sum(by_a * wide, -1, keepdims=True) * (scale * scale * scale) * (1.0 / d)
             d_out[lax.rem(i, RING)] = by + (by_a * scale - wide * inner).astype(BF16)
             back(i).start()
 
-        pl.when(me > 0)(send) if recompute else send()
-
-    def out_copies(slot, p):
-        here = pl.ds(p * (d // PARTS), d // PARTS)
-        return [
-            pltpu.make_async_copy(buf.at[slot, here, :], out.at[here, :], o_sem.at[k, p])
-            for k, (buf, out) in enumerate(((dg, og), (du, ou), (act, od)))
-        ]
-
-    def weigh(m, p):
+    def weigh(m, p, final):
         slot = lax.rem(m, 2)
         here = pl.ds(pl.multiple_of(p * (d // PARTS), d // PARTS), d // PARTS)
-        for left, right, acc in ((at, dg, acc_g), (at, du, acc_u), (byt, act, acc_d)):
+        for left, right, acc, out in ((at, dg, acc_g, wg), (at, du, acc_u, wu), (byt, act, acc_d, wd)):
             lhs = left[slot, here, :]
             for j in range(0, ff, COLS):
                 cols = pl.ds(j, COLS)
-                acc[here, cols] += dot(lhs, right[slot, :, cols]).astype(BF16).astype(F32)
-
-        @pl.when(m == n // pieces - 1)
-        def _():
-            for acc, buf in ((acc_g, dg), (acc_u, du), (acc_d, act)):
-                buf[1 - slot, here, :] = acc[here, :].astype(BF16)
-            for copy in out_copies(1 - slot, p):
-                copy.start()
+                total = acc[here, cols] + dot(lhs, right[slot, :, cols]).astype(BF16).astype(F32)
+                if not final:
+                    acc[here, cols] = total
+                elif out is wd:
+                    out[cols, here] = total.astype(BF16).T
+                else:
+                    out[here, cols] = total.astype(BF16)
 
     def step(i, carry):
-        @pl.when((me < stages - 1) & (i < n))
-        def _():
-            forward(i)
-
-        @pl.when(i == jnp.where(first, 1, 0))
+        @pl.when(i == jnp.where(first, 2, 0))
         def _():
             for j in range(0, ff, COLS):
                 wdt[:, j : j + COLS] = wd[j : j + COLS, :].T
@@ -210,21 +203,35 @@
                     wgt[j : j + COLS, :] = wg[:, j : j + COLS].T
                     wut[j : j + COLS, :] = wu[:, j : j + COLS].T
 
+        @pl.when((me < stages - 1) & (i < n))
+        def _():
+            forward(i)
+
         ib = i - lag
 
         @pl.when((ib >= 0) & (ib < n) & middle)
         def _():
-            backward(ib, False)
-
-        @pl.when((ib >= 0) & (ib < n) & ~middle)
-        def _():
-            backward(ib, True)
+            backward(ib, False, True)
+
+        @pl.when((ib >= 0) & (ib < n) & last)
+        def _():
+            backward(ib, True, True)
+
+        @pl.when((ib >= 0) & (ib < n) & first)
+        def _():
+            backward(ib, True, False)
 
         iw, every = ib - pieces, pieces // PARTS
-
-        @pl.when((iw >= 0) & (lax.rem(iw + pieces, every) == every - 1))
-        def _():
-            weigh(lax.div(iw, pieces), lax.div(lax.rem(iw, pieces), every))
+        turn = (iw >= 0) & (lax.rem(iw + pieces, every) == every - 1)
+        mw, pw = lax.div(iw, pieces), lax.div(lax.rem(iw, pieces), every)
+
+        @pl.when(turn & (iw < n - pieces))
+        def _():
+            weigh(mw, pw, False)
+
+        @pl.when(turn & (iw >= n - pieces))
+        def _():
+            weigh(mw, pw, True)
 
         return carry
 
@@ -237,11 +244,6 @@
     @pl.when(me > 0)
     def _():
         lax.fori_loop(n - RING, n, lambda i, c: (back(i).wait_send(), c)[1], 0)
-
-    free = (n // pieces) % 2
-    for p in range(PARTS):
-        for copy in out_copies(free, p):
-            copy.wait()
 
 
 def solution(mesh):
@@ -258,23 +260,22 @@
         og, ou, od = pl.pallas_call(
             functools.partial(kernel, stages, pieces),
             name="pipeline",
-            out_shape=[jax.ShapeDtypeStruct((d, ff), BF16)] * 3,
+            out_shape=[pltpu.VMEM(shape, BF16) for shape in ((d, ff), (d, ff), (ff, d))],
             in_specs=[pl.BlockSpec(memory_space=pltpu.HBM)] * 5,
-            out_specs=[pl.BlockSpec(memory_space=pltpu.HBM)] * 3,
+            out_specs=[pl.BlockSpec(memory_space=pltpu.VMEM)] * 3,
             scratch_shapes=[
-                vmem(d, ff), vmem(d, ff), vmem(ff, d), vmem(ff, d), vmem(ff, d), vmem(d, ff),
+                vmem(ff, d), vmem(ff, d), vmem(d, ff),
                 *[vmem(d, ff, dtype=F32)] * 3,
                 *[vmem(n, ROWS, d)] * 2,
                 *[vmem(RING, ROWS, d)] * 2,
-                vmem(ROWS, ff),
                 *[vmem(max(stages - 2, 0) * LAG + 1, ROWS, ff, dtype=F32)] * 2,
                 *[vmem(2, tokens, ff)] * 3,
                 vmem(2, d, tokens), vmem(2, d, tokens),
-                sems(3), sems(3, PARTS), sems(n), sems(n), sems(n), sems(n),
+                sems(3), sems(n), sems(n), sems(n), sems(n),
             ],
-            compiler_params=pltpu.CompilerParams(collective_id=0, has_side_effects=True, vmem_limit_bytes=67_000_000),
+            compiler_params=pltpu.CompilerParams(collective_id=0, has_side_effects=True, vmem_limit_bytes=60_500_000),
         )(chunks(x), chunks(dy), w_gate[0], w_up[0], w_down[0])
-        return og[None], ou[None], od.T[None]
+        return og[None], ou[None], od[None]
 
     return jax.shard_map(
         step,

time: 154 us -> 182 us (1.18)
  Pallas kernels: 146 us -> 178 us
  local copies, waits for them, and re-layouts: 7.36 us -> 3.69 us
    pallas_call x1, Pallas kernels: 146 us -> 178 us  [step(): pl.pallas_call(functools.partial(kernel, stages, pieces), name='pipeline'...]
    unnamed x7 -> x3, local copies, waits for them, and re-layouts: 7.36 us -> 3.69 us
where the time goes in v2:
time: 182 us
  Pallas kernels  178 us (98%)
  local copies, waits for them, and re-layouts  3.69 us (2%)
    pallas_call x1, Pallas kernels, step(): pl.pallas_call(functools.partial(kernel, stages, pieces), name='pipeline'...  178 us
    unnamed x3, local copies, waits for them, and re-layouts  3.69 us

profile of v2, /device:TPU:120, one launch (start us, length us, event | category | flops | bytes accessed | tf_op | source)
XLA Modules:
  0.0 182.2 jit_solution(281317550043198570)
XLA Ops:
  0.6 177.9 %pipeline.1 = (bf16[512,1792]{1,0:T(8,128)(2,1)S(1)}, bf16[512,1792]{1,0:T(8,128)(2,1)S(1)}, bf16[1792,512]{1,0:T(8,128)(2,1)S(1)}) custom-call(bf16[32,128,512]{2,1,0:T(8,128)(2,1)} %bitcast.11, bf16[32,128,512]{2,1,0:T(8,128)(2,1)} %bitcast.12, bf16[512,1792]{1,0:T(8,128)(2,1)} %bitcast.13, bf16[512,1792]{1,0:T(8,128)(2,1)} %bitcast.14, ...), custom_call_target="tpu_custom_call" | custom-call | tf_op jit(solution)/shard_map/pipeline/pallas_call | solution.py:260
  178.5 1.2 copy.11
  179.8 1.2 copy.12
  181.0 1.2 copy.13

commit v3 on v2

--- a/solution.py
+++ b/solution.py
@@ -25,7 +25,7 @@
     x, dy, wg_in, wu_in, wd_in,
     wg, wu, wd,
     wgt, wut, wdt, acc_g, acc_u, acc_d,
-    h_in, d_in, h_out, d_out, kept_g, kept_u, act, dg, du, at, byt,
+    h_in, d_in, h_out, d_out, fact, kept_g, kept_u, act, dg, du, at, byt,
     w_sem, rf, rb, sf, sb,
 ):
     me = lax.axis_index("pp")
@@ -120,14 +120,13 @@
 
         _, _, a = normed(i)
         spot = lax.rem(i, keeps)
-        y = 0.0
         for j in range(0, ff, COLS):
             cols = pl.ds(j, COLS)
             gate, up = dot(a, wg[:, cols]), dot(a, wu[:, cols])
             kept_g[spot, :, cols] = gate
             kept_u[spot, :, cols] = up
-            y += dot((gate * jax.nn.sigmoid(gate) * up).astype(BF16), wd[cols, :])
-        y = y.astype(BF16)
+            fact[:, cols] = (gate * jax.nn.sigmoid(gate) * up).astype(BF16)
+        y = dot(fact[...], wd[...]).astype(BF16)
         h_out[lax.rem(i, RING)] = h_in[i] + y
         onward(i).start()
 
@@ -150,14 +149,16 @@
         by = d_in[i]
         at[slot, :, here] = a.T
         byt[slot, :, here] = by.T
-        by_a_g, by_a_u = 0.0, 0.0
+        firsts = []
         for j in range(0, ff, COLS):
             cols = pl.ds(j, COLS)
-            if recompute:
-                gate, up = dot(a, wg[:, cols]), dot(a, wu[:, cols])
-            else:
-                gate, up = kept_g[spot, :, cols], kept_u[spot, :, cols]
-            by_act = dot(by, wdt[:, cols]).astype(BF16).astype(F32)
+            gate_up = (dot(a, wg[:, cols]), dot(a, wu[:, cols])) if recompute else ()
+            firsts.append((*gate_up, dot(by, wdt[:, cols])))
+        by_a_g, by_a_u = 0.0, 0.0
+        for j, (*gate_up, by_act) in zip(range(0, ff, COLS), firsts, strict=True):
+            cols = pl.ds(j, COLS)
+            gate, up = gate_up if recompute else (kept_g[spot, :, cols], kept_u[spot, :, cols])
+            by_act = by_act.astype(BF16).astype(F32)
             sg = jax.nn.sigmoid(gate)
             silu = gate * sg
             by_up = (by_act * silu).astype(BF16)
@@ -268,6 +269,7 @@
                 *[vmem(d, ff, dtype=F32)] * 3,
                 *[vmem(n, ROWS, d)] * 2,
                 *[vmem(RING, ROWS, d)] * 2,
+                vmem(ROWS, ff),
                 *[vmem(max(stages - 2, 0) * LAG + 1, ROWS, ff, dtype=F32)] * 2,
                 *[vmem(2, tokens, ff)] * 3,
                 vmem(2, d, tokens), vmem(2, d, tokens),

time: 182 us -> 145 us (0.80)
  Pallas kernels: 178 us -> 141 us
    pallas_call x1, Pallas kernels: 178 us -> 141 us  [step(): pl.pallas_call(functools.partial(kernel, stages, pieces), name='pipeline'...]
where the time goes in v3:
time: 145 us
  Pallas kernels  141 us (97%)
  local copies, waits for them, and re-layouts  3.69 us (3%)
    pallas_call x1, Pallas kernels, step(): pl.pallas_call(functools.partial(kernel, stages, pieces), name='pipeline'...  141 us
    unnamed x3, local copies, waits for them, and re-layouts  3.69 us

profile of v3, /device:TPU:120, one launch (start us, length us, event | category | flops | bytes accessed | tf_op | source)
XLA Modules:
  0.0 145.3 jit_solution(11635561905615987022)
XLA Ops:
  0.6 140.9 %pipeline.1 = (bf16[512,1792]{1,0:T(8,128)(2,1)S(1)}, bf16[512,1792]{1,0:T(8,128)(2,1)S(1)}, bf16[1792,512]{1,0:T(8,128)(2,1)S(1)}) custom-call(bf16[32,128,512]{2,1,0:T(8,128)(2,1)} %bitcast.11, bf16[32,128,512]{2,1,0:T(8,128)(2,1)} %bitcast.12, bf16[512,1792]{1,0:T(8,128)(2,1)} %bitcast.13, bf16[512,1792]{1,0:T(8,128)(2,1)} %bitcast.14, ...), custom_call_target="tpu_custom_call" | custom-call | tf_op jit(solution)/shard_map/pipeline/pallas_call | solution.py:261
  141.6 1.2 copy.11
  142.8 1.2 copy.12
  144.0 1.2 copy.13

commit v4 on v2

v4 whole, which is shorter than its diff:
```python
import functools

import jax
import jax.numpy as jnp
from jax import lax
from jax.experimental import pallas as pl
from jax.experimental.pallas import tpu as pltpu
from jax.sharding import PartitionSpec as P

ROWS = 128
PARTS = 2
COLS = 256
RING = 3
LAG = 4
MESH = pl.DeviceIdType.MESH
F32, BF16 = jnp.float32, jnp.bfloat16


def dot(a, b):
    return jnp.dot(a, b, preferred_element_type=F32)


def kernel(
    stages, pieces,
    x, dy, wg_in, wu_in, wd_in,
    wg, wu, wd,
    wgt, wut, wdt, acc_g, acc_u, acc_d,
    h_in, d_in, h_out, kept_s, kept_q, act, dg, du, at, byt,
    w_sem, rf, rb, sf, sb,
):
    me = lax.axis_index("pp")
    n, rows, d = x.shape
    ff = wg_in.shape[1]
    first, last = me == 0, me == stages - 1
    middle = (me > 0) & (me < stages - 1)
    keeps = kept_s.shape[0]
    lag = (stages - 1 - me) * LAG

    def load_x(i):
        return pltpu.make_async_copy(x.at[i], h_in.at[i], rf.at[i])

    def load_dy(i):
        return pltpu.make_async_copy(dy.at[i], d_in.at[i], rb.at[i])

    tiles = range(0, ff, COLS)

    def load_w(k, j):
        src, dst = ((wg_in, wg), (wu_in, wu), (wd_in, wd))[k]
        part = (pl.ds(j, COLS), slice(None)) if k == 2 else (slice(None), pl.ds(j, COLS))
        return pltpu.make_async_copy(src.at[part], dst.at[part], w_sem.at[k, j // COLS])

    @pl.when(first)
    def _():
        load_x(0).start()

    for j in tiles:
        load_w(0, j).start()
        load_w(1, j).start()
    for j in tiles:
        load_w(2, j).start()

    @pl.when(first)
    def _():
        lax.fori_loop(1, n, lambda i, c: (load_x(i).start(), c)[1], 0)

    @pl.when(last)
    def _():
        lax.fori_loop(0, n, lambda i, c: (load_dy(i).start(), c)[1], 0)

    def onward(i):
        return pltpu.make_async_remote_copy(
            src_ref=h_out.at[lax.rem(i, RING)], dst_ref=h_in.at[i], send_sem=sf.at[i], recv_sem=rf.at[i],
            device_id={"pp": jnp.minimum(me + 1, stages - 1)}, device_id_type=MESH,
        )

    def back(i):
        return pltpu.make_async_remote_copy(
            src_ref=d_in.at[i], dst_ref=d_in.at[i], send_sem=sb.at[i], recv_sem=rb.at[i],
            device_id={"pp": jnp.maximum(me - 1, 0)}, device_id_type=MESH,
        )

    barrier = pltpu.get_barrier_semaphore()

    @pl.when(me > 0)
    def _():
        pl.semaphore_signal(barrier, inc=1, device_id={"pp": me - 1}, device_id_type=MESH)

    @pl.when(me < stages - 1)
    def _():
        pl.semaphore_signal(barrier, inc=1, device_id={"pp": me + 1}, device_id_type=MESH)

    pl.semaphore_wait(barrier, (me > 0).astype(jnp.int32) + (me < stages - 1).astype(jnp.int32))

    @pl.when(me > 0)
    def _():
        for j in tiles:
            for k in range(3):
                load_w(k, j).wait()

    def wait_h(i):
        @pl.when(first)
        def _():
            load_x(i).wait()

        @pl.when(me > 0)
        def _():
            onward(i).wait_recv()

    def wait_d(i):
        @pl.when(last)
        def _():
            load_dy(i).wait()

        @pl.when(me < stages - 1)
        def _():
            back(i).wait_recv()

    def normed(i):
        wide = h_in[i].astype(F32)
        scale = lax.rsqrt(jnp.mean(wide * wide, -1, keepdims=True) + 1e-6)
        return wide, scale, (wide * scale).astype(BF16)

    def place(i):
        m, c = lax.div(i, pieces), lax.rem(i, pieces)
        return lax.rem(m, 2), lax.rem(m, act.shape[0]), pl.ds(pl.multiple_of(c * rows, rows), rows)

    def forward(i, start):
        wait_h(i)
        if not start:

            @pl.when(i >= RING)
            def _():
                onward(i - RING).wait_send()

        _, _, a = normed(i)
        spot = lax.rem(i, keeps)
        _, slot, here = place(jnp.where(first, i + 2 * pieces, i))
        for j in tiles:
            cols = pl.ds(j, COLS)
            if start:
                load_w(0, j).wait()
                load_w(1, j).wait()

            gate, up = dot(a, wg[:, cols]), dot(a, wu[:, cols])
            sg = jax.nn.sigmoid(gate)
            silu = gate * sg
            kept_s[spot, :, cols] = silu
            kept_q[spot, :, cols] = up * (sg + silu * (1.0 - sg))
            act[slot, here, cols] = (silu * up).astype(BF16)
        if start:
            for j in tiles:
                load_w(2, j).wait()

        y = dot(act[slot, here, :], wd[...]).astype(BF16)
        h_out[lax.rem(i, RING)] = h_in[i] + y
        onward(i).start()

    def backward(i, recompute, send):
        @pl.when(last)
        def _():
            wait_h(i)

        wait_d(i)
        slot, act_slot, here = place(i)
        spot = lax.rem(i, keeps)
        wide, scale, a = normed(i)
        by = d_in[i]
        at[slot, :, here] = a.T
        byt[slot, :, here] = by.T
        if recompute:
            for j in tiles:
                cols = pl.ds(j, COLS)
                gate, up = dot(a, wg[:, cols]), dot(a, wu[:, cols])
                by_act = dot(by, wdt[:, cols]).astype(BF16).astype(F32)
                sg = jax.nn.sigmoid(gate)
                silu = gate * sg
                act[act_slot, here, cols] = (silu * up).astype(BF16)
                du[slot, here, cols] = (by_act * silu).astype(BF16)
                dg[slot, here, cols] = (by_act * (up * (sg + silu * (1.0 - sg)))).astype(BF16)
            if send:
                by_a_g, by_a_u = dot(dg[slot, here, :], wgt[...]), dot(du[slot, here, :], wut[...])
        else:
            by_a_g, by_a_u = 0.0, 0.0
            firsts = [dot(by, wdt[:, pl.ds(j, COLS)]) for j in tiles]
            for j, by_act in zip(tiles, firsts, strict=True):
                cols = pl.ds(j, COLS)
                by_act = by_act.astype(BF16).astype(F32)
                by_up = (by_act * kept_s[spot, :, cols]).astype(BF16)
                by_gate = (by_act * kept_q[spot, :, cols]).astype(BF16)
                du[slot, here, cols] = by_up
                dg[slot, here, cols] = by_gate
                by_a_g += dot(by_gate, wgt[cols, :])
                by_a_u += dot(by_up, wut[cols, :])
        if send:
            by_a = (by_a_g.astype(BF16) + by_a_u.astype(BF16)).astype(F32)
            inner = jnp.sum(by_a * wide, -1, keepdims=True) * (scale * scale * scale) * (1.0 / d)
            d_in[i] = by + (by_a * scale - wide * inner).astype(BF16)
            back(i).start()

    jobs = [(k, j) for k in range(3) for j in tiles]
    sets = pieces // PARTS

    def weigh(m, p, e, final):
        slot, act_slot = lax.rem(m, 2), lax.rem(m, act.shape[0])
        here = pl.ds(pl.multiple_of(p * (d // PARTS), d // PARTS), d // PARTS)
        for k, j in jobs[e * len(jobs) // sets : (e + 1) * len(jobs) // sets]:
            cols = pl.ds(j, COLS)
            lhs = (at, at, byt)[k][slot, here, :]
            rhs = act[act_slot, :, cols] if k == 2 else (dg, du)[k][slot, :, cols]
            acc, out = (acc_g, acc_u, acc_d)[k], (wg, wu, wd)[k]
            total = acc[here, cols] + dot(lhs, rhs).astype(BF16).astype(F32)
            if not final:
                acc[here, cols] = total
            elif k == 2:
                out[cols, here] = total.astype(BF16).T
            else:
                out[here, cols] = total.astype(BF16)

    def step(i, carry):
        @pl.when(i == jnp.where(first, 3, 0))
        def _():
            for j in tiles:
                wdt[:, j : j + COLS] = wd[j : j + COLS, :].T
            for acc in (acc_g, acc_u, acc_d):
                acc[...] = jnp.zeros_like(acc)

            @pl.when(me > 0)
            def _():
                for j in tiles:
                    wgt[j : j + COLS, :] = wg[:, j : j + COLS].T
                    wut[j : j + COLS, :] = wu[:, j : j + COLS].T

        @pl.when(first & (i == 0))
        def _():
            forward(i, True)

        @pl.when((me < stages - 1) & (i + me > 0) & (i < n))
        def _():
            forward(i, False)

        ib = i - lag

        @pl.when((ib >= 0) & (ib < n) & middle)
        def _():
            backward(ib, False, True)

        @pl.when((ib >= 0) & (ib < n) & last)
        def _():
            backward(ib, True, True)

        @pl.when((ib >= 0) & (ib < n) & first)
        def _():
            backward(ib, True, False)

        iw = ib - pieces
        mw, pw = lax.div(iw, pieces), lax.div(lax.rem(iw, pieces), sets)
        for e in range(sets):
            turn = (iw >= 0) & (lax.rem(iw + pieces, sets) == e)

            @pl.when(turn & (iw < n - pieces))
            def _():
                weigh(mw, pw, e, False)

            @pl.when(turn & (iw >= n - pieces))
            def _():
                weigh(mw, pw, e, True)

        return carry

    lax.fori_loop(0, n + lag + pieces, step, 0)

    @pl.when(me < stages - 1)
    def _():
        lax.fori_loop(n - RING, n, lambda i, c: (onward(i).wait_send(), c)[1], 0)

    @pl.when(me > 0)
    def _():
        lax.fori_loop(0, n, lambda i, c: (back(i).wait_send(), c)[1], 0)


def solution(mesh):
    stages = mesh.shape["pp"]

    def step(x, dy, w_gate, w_up, w_down):
        micro, tokens, d = x.shape
        ff = w_gate.shape[2]
        pieces = tokens // ROWS
        n = micro * pieces
        chunks = lambda v: v.reshape(n, ROWS, d)
        vmem = lambda *shape, dtype=BF16: pltpu.VMEM(shape, dtype)
        sems = lambda *shape: pltpu.SemaphoreType.DMA(shape)
        og, ou, od = pl.pallas_call(
            functools.partial(kernel, stages, pieces),
            name="pipeline",
            out_shape=[pltpu.VMEM(shape, BF16) for shape in ((d, ff), (d, ff), (ff, d))],
            in_specs=[pl.BlockSpec(memory_space=pltpu.HBM)] * 5,
            out_specs=[pl.BlockSpec(memory_space=pltpu.VMEM)] * 3,
            scratch_shapes=[
                vmem(ff, d), vmem(ff, d), vmem(d, ff),
                *[vmem(d, ff, dtype=F32)] * 3,
                *[vmem(n, ROWS, d)] * 2,
                vmem(RING, ROWS, d),
                *[vmem(max(stages - 2, 0) * LAG + 1, ROWS, ff, dtype=F32)] * 2,
                vmem(4, tokens, ff), *[vmem(2, tokens, ff)] * 2,
                vmem(2, d, tokens), vmem(2, d, tokens),
                sems(3, ff // COLS), sems(n), sems(n), sems(n), sems(n),
            ],
            compiler_params=pltpu.CompilerParams(collective_id=0, has_side_effects=True, vmem_limit_bytes=61_500_000),
        )(chunks(x), chunks(dy), w_gate[0], w_up[0], w_down[0])
        return og[None], ou[None], od[None]

    return jax.shard_map(
        step,
        mesh=mesh,
        in_specs=(P("rep", None, None),) * 2 + (P("pp", None, None),) * 3,
        out_specs=(P(("rep", "pp"), None, None),) * 3,
        check_vma=False,
    )
```

time: 182 us -> 143 us (0.79)
  Pallas kernels: 178 us -> 138 us
    pallas_call x1, Pallas kernels: 178 us -> 138 us  [step(): pl.pallas_call(functools.partial(kernel, stages, pieces), name='pipeline'...]
where the time goes in v4:
time: 143 us
  Pallas kernels  138 us (97%)
  local copies, waits for them, and re-layouts  3.69 us (3%)
    pallas_call x1, Pallas kernels, step(): pl.pallas_call(functools.partial(kernel, stages, pieces), name='pipeline'...  138 us
    unnamed x3, local copies, waits for them, and re-layouts  3.69 us

profile of v4, /device:TPU:120, one launch (start us, length us, event | category | flops | bytes accessed | tf_op | source)
XLA Modules:
  0.0 142.6 jit_solution(3859845469538138937)
XLA Ops:
  0.6 138.3 %pipeline.1 = (bf16[512,1792]{1,0:T(8,128)(2,1)S(1)}, bf16[512,1792]{1,0:T(8,128)(2,1)S(1)}, bf16[1792,512]{1,0:T(8,128)(2,1)S(1)}) custom-call(bf16[32,128,512]{2,1,0:T(8,128)(2,1)} %bitcast.11, bf16[32,128,512]{2,1,0:T(8,128)(2,1)} %bitcast.12, bf16[512,1792]{1,0:T(8,128)(2,1)} %bitcast.13, bf16[512,1792]{1,0:T(8,128)(2,1)} %bitcast.14, ...), custom_call_target="tpu_custom_call" | custom-call | tf_op jit(solution)/shard_map/pipeline/pallas_call | solution.py:292
  139.0 1.2 copy.11
  140.2 1.2 copy.12
  141.4 1.2 copy.13

commit v5 on v4

--- a/solution.py
+++ b/solution.py
@@ -216,6 +216,29 @@
             else:
                 out[here, cols] = total.astype(BF16)
 
+    def weigh_half(h):
+        m, half = n // pieces - 1, pieces * rows // 2
+        part, slots = pl.ds(h * half, half), d // rows
+        for k, j in sorted(jobs, reverse=True):
+            cols = pl.ds(j, COLS)
+            left = (at, at, byt)[k].at[m % 2]
+            right = act.at[m % act.shape[0]] if k == 2 else (dg, du)[k].at[m % 2]
+            acc, out = (acc_g, acc_u, acc_d)[k], (wg, wu, wd)[k]
+            kept, first_spot = (kept_s, kept_s, kept_q)[k], (0, slots, 0)[k]
+            for p in range(0, d, d // PARTS):
+                term = dot(left[pl.ds(p, d // PARTS), part], right[part, cols])
+                for r in range(0, d // PARTS, rows):
+                    here, spot, one = pl.ds(p + r, rows), first_spot + (p + r) // rows, term[r : r + rows]
+                    if h == 0:
+                        kept[spot, :, cols] = one
+                    else:
+                        one = (kept[spot, :, cols] + one).astype(BF16).astype(F32)
+                        total = (acc[here, cols] + one).astype(BF16)
+                        if k == 2:
+                            out[cols, here] = total.T
+                        else:
+                            out[here, cols] = total
+
     def step(i, carry):
         @pl.when(i == jnp.where(first, 3, 0))
         def _():
@@ -252,22 +275,38 @@
         def _():
             backward(ib, True, False)
 
-        iw = ib - pieces
-        mw, pw = lax.div(iw, pieces), lax.div(lax.rem(iw, pieces), sets)
-        for e in range(sets):
-            turn = (iw >= 0) & (lax.rem(iw + pieces, sets) == e)
-
-            @pl.when(turn & (iw < n - pieces))
-            def _():
-                weigh(mw, pw, e, False)
-
-            @pl.when(turn & (iw >= n - pieces))
-            def _():
-                weigh(mw, pw, e, True)
+        hurry = first & (ib >= n - pieces)
+        start = jnp.where(hurry, n - 2 * pieces + 2 * (ib - n + pieces), ib - pieces)
+        count = jnp.where(hurry, jnp.where(ib < n - pieces // 2, 2, 0), jnp.where(ib >= pieces, 1, 0))
+
+        def weigh_part(iw, carry):
+            mw, pw = lax.div(iw, pieces), lax.div(lax.rem(iw, pieces), sets)
+            for e in range(sets):
+                turn = lax.rem(iw, sets) == e
+
+                @pl.when(turn & (iw < n - pieces))
+                def _():
+                    weigh(mw, pw, e, False)
+
+                @pl.when(turn & (iw >= n - pieces))
+                def _():
+                    weigh(mw, pw, e, True)
+
+            return carry
+
+        lax.fori_loop(start, start + count, weigh_part, 0)
+
+        @pl.when(first & (ib == n - pieces // 2))
+        def _():
+            weigh_half(0)
+
+        @pl.when(first & (ib == n - 1))
+        def _():
+            weigh_half(1)
 
         return carry
 
-    lax.fori_loop(0, n + lag + pieces, step, 0)
+    lax.fori_loop(0, n + lag + jnp.where(first, 0, pieces), step, 0)
 
     @pl.when(me < stages - 1)
     def _():

time: 143 us -> 141 us (0.986)
  no operation moved by 1% of the time
where the time goes in v5:
time: 141 us
  Pallas kernels  137 us (97%)
  local copies, waits for them, and re-layouts  3.69 us (3%)
    pallas_call x1, Pallas kernels, step(): pl.pallas_call(functools.partial(kernel, stages, pieces), name='pipeline'...  137 us
    unnamed x3, local copies, waits for them, and re-layouts  3.69 us

profile of v5, /device:TPU:120, one launch (start us, length us, event | category | flops | bytes accessed | tf_op | source)
XLA Modules:
  0.0 141.4 jit_solution(6960946419897133042)
XLA Ops:
  0.6 137.0 %pipeline.1 = (bf16[512,1792]{1,0:T(8,128)(2,1)S(1)}, bf16[512,1792]{1,0:T(8,128)(2,1)S(1)}, bf16[1792,512]{1,0:T(8,128)(2,1)S(1)}) custom-call(bf16[32,128,512]{2,1,0:T(8,128)(2,1)} %bitcast.11, bf16[32,128,512]{2,1,0:T(8,128)(2,1)} %bitcast.12, bf16[512,1792]{1,0:T(8,128)(2,1)} %bitcast.13, bf16[512,1792]{1,0:T(8,128)(2,1)} %bitcast.14, ...), custom_call_target="tpu_custom_call" | custom-call | tf_op jit(solution)/shard_map/pipeline/pallas_call | solution.py:331
  137.7 1.2 copy.11
  138.9 1.2 copy.12
  140.1 1.2 copy.13

commit v6 on v5

--- a/solution.py
+++ b/solution.py
@@ -154,6 +154,10 @@
         y = dot(act[slot, here, :], wd[...]).astype(BF16)
         h_out[lax.rem(i, RING)] = h_in[i] + y
         onward(i).start()
+        if not start:
+            @pl.when(first & (i == n - 1))
+            def _():
+                kept_q[keeps - 1] = act[slot, here, :].astype(F32)
 
     def backward(i, recompute, send):
         @pl.when(last)
@@ -177,21 +181,16 @@
                 act[act_slot, here, cols] = (silu * up).astype(BF16)
                 du[slot, here, cols] = (by_act * silu).astype(BF16)
                 dg[slot, here, cols] = (by_act * (up * (sg + silu * (1.0 - sg)))).astype(BF16)
-            if send:
-                by_a_g, by_a_u = dot(dg[slot, here, :], wgt[...]), dot(du[slot, here, :], wut[...])
         else:
-            by_a_g, by_a_u = 0.0, 0.0
-            firsts = [dot(by, wdt[:, pl.ds(j, COLS)]) for j in tiles]
-            for j, by_act in zip(tiles, firsts, strict=True):
+            for j in tiles:
                 cols = pl.ds(j, COLS)
-                by_act = by_act.astype(BF16).astype(F32)
-                by_up = (by_act * kept_s[spot, :, cols]).astype(BF16)
-                by_gate = (by_act * kept_q[spot, :, cols]).astype(BF16)
-                du[slot, here, cols] = by_up
-                dg[slot, here, cols] = by_gate
-                by_a_g += dot(by_gate, wgt[cols, :])
-                by_a_u += dot(by_up, wut[cols, :])
+                by_act = dot(by, wdt[:, cols]).astype(BF16).astype(F32)
+                du[slot, here, cols] = (by_act * kept_s[spot, :, cols]).astype(BF16)
+                dg[slot, here, cols] = (by_act * kept_q[spot, :, cols]).astype(BF16)
+                if not send:
+                    act[act_slot, here, cols] = kept_q[keeps - 1, :, cols].astype(BF16)
         if send:
+            by_a_g, by_a_u = dot(dg[slot, here, :], wgt[...]), dot(du[slot, here, :], wut[...])
             by_a = (by_a_g.astype(BF16) + by_a_u.astype(BF16)).astype(F32)
             inner = jnp.sum(by_a * wide, -1, keepdims=True) * (scale * scale * scale) * (1.0 / d)
             d_in[i] = by + (by_a * scale - wide * inner).astype(BF16)
@@ -225,10 +224,12 @@
             right = act.at[m % act.shape[0]] if k == 2 else (dg, du)[k].at[m % 2]
             acc, out = (acc_g, acc_u, acc_d)[k], (wg, wu, wd)[k]
             kept, first_spot = (kept_s, kept_s, kept_q)[k], (0, slots, 0)[k]
+            taken = (n - 1) % keeps
             for p in range(0, d, d // PARTS):
                 term = dot(left[pl.ds(p, d // PARTS), part], right[part, cols])
                 for r in range(0, d // PARTS, rows):
                     here, spot, one = pl.ds(p + r, rows), first_spot + (p + r) // rows, term[r : r + rows]
+                    spot += spot >= taken
                     if h == 0:
                         kept[spot, :, cols] = one
                     else:
@@ -271,9 +272,13 @@
         def _():
             backward(ib, True, True)
 
-        @pl.when((ib >= 0) & (ib < n) & first)
+        @pl.when((ib >= 0) & (ib < n - 1) & first)
         def _():
             backward(ib, True, False)
+
+        @pl.when((ib == n - 1) & first)
+        def _():
+            backward(ib, False, False)
 
         hurry = first & (ib >= n - pieces)
         start = jnp.where(hurry, n - 2 * pieces + 2 * (ib - n + pieces), ib - pieces)

time: 141 us -> 141 us (level)
  no operation moved by 1% of the time
where the time goes in v6:
time: 141 us
  Pallas kernels  136 us (96%)
  local copies, waits for them, and re-layouts  3.69 us (3%)
    pallas_call x1, Pallas kernels, step(): pl.pallas_call(functools.partial(kernel, stages, pieces), name='pipeline'...  136 us
    unnamed x3, local copies, waits for them, and re-layouts  3.69 us

profile of v6, /device:TPU:120, one launch (start us, length us, event | category | flops | bytes accessed | tf_op | source)
XLA Modules:
  0.0 140.6 jit_solution(16659140423727889391)
XLA Ops:
  0.6 136.3 %pipeline.1 = (bf16[512,1792]{1,0:T(8,128)(2,1)S(1)}, bf16[512,1792]{1,0:T(8,128)(2,1)S(1)}, bf16[1792,512]{1,0:T(8,128)(2,1)S(1)}) custom-call(bf16[32,128,512]{2,1,0:T(8,128)(2,1)} %bitcast.11, bf16[32,128,512]{2,1,0:T(8,128)(2,1)} %bitcast.12, bf16[512,1792]{1,0:T(8,128)(2,1)} %bitcast.13, bf16[512,1792]{1,0:T(8,128)(2,1)} %bitcast.14, ...), custom_call_target="tpu_custom_call" | custom-call | tf_op jit(solution)/shard_map/pipeline/pallas_call | solution.py:336
  136.9 1.2 copy.11
  138.2 1.2 copy.12
  139.4 1.2 copy.13

commit v7 on v6

--- a/solution.py
+++ b/solution.py
@@ -34,7 +34,7 @@
     first, last = me == 0, me == stages - 1
     middle = (me > 0) & (me < stages - 1)
     keeps = kept_s.shape[0]
-    lag = (stages - 1 - me) * LAG
+    lag = (stages - 1 - me) * LAG + jnp.where(first, 2, 0)
 
     def load_x(i):
         return pltpu.make_async_copy(x.at[i], h_in.at[i], rf.at[i])
@@ -52,16 +52,13 @@
     @pl.when(first)
     def _():
         load_x(0).start()
+        load_x(1).start()
 
     for j in tiles:
         load_w(0, j).start()
         load_w(1, j).start()
     for j in tiles:
         load_w(2, j).start()
-
-    @pl.when(first)
-    def _():
-        lax.fori_loop(1, n, lambda i, c: (load_x(i).start(), c)[1], 0)
 
     @pl.when(last)
     def _():
@@ -257,6 +254,7 @@
         @pl.when(first & (i == 0))
         def _():
             forward(i, True)
+            lax.fori_loop(2, n, lambda i, c: (load_x(i).start(), c)[1], 0)
 
         @pl.when((me < stages - 1) & (i + me > 0) & (i < n))
         def _():

time: 141 us -> 141 us (level)
  no operation moved by 1% of the time
where the time goes in v7:
time: 141 us
  Pallas kernels  136 us (96%)
  local copies, waits for them, and re-layouts  3.69 us (3%)
    pallas_call x1, Pallas kernels, step(): pl.pallas_call(functools.partial(kernel, stages, pieces), name='pipeline'...  136 us
    unnamed x3, local copies, waits for them, and re-layouts  3.69 us

profile of v7, /device:TPU:120, one launch (start us, length us, event | category | flops | bytes accessed | tf_op | source)
XLA Modules:
  0.0 140.6 jit_solution(17547867881720092096)
XLA Ops:
  0.6 136.2 %pipeline.1 = (bf16[512,1792]{1,0:T(8,128)(2,1)S(1)}, bf16[512,1792]{1,0:T(8,128)(2,1)S(1)}, bf16[1792,512]{1,0:T(8,128)(2,1)S(1)}) custom-call(bf16[32,128,512]{2,1,0:T(8,128)(2,1)} %bitcast.11, bf16[32,128,512]{2,1,0:T(8,128)(2,1)} %bitcast.12, bf16[512,1792]{1,0:T(8,128)(2,1)} %bitcast.13, bf16[512,1792]{1,0:T(8,128)(2,1)} %bitcast.14, ...), custom_call_target="tpu_custom_call" | custom-call | tf_op jit(solution)/shard_map/pipeline/pallas_call | solution.py:334
  136.9 1.2 copy.11
  138.1 1.2 copy.12
  139.3 1.2 copy.13
